TPU v7x, 32 devices: a whole 2x2x4 slice. The times are simulated.
32 devices in a mesh: ta: 4 (over x, core), tb: 8 (over z, y).
Axes of the slice: x: 2, y: 2, z: 4, core: 2. Of those that a mesh axis runs over, the one named last changes fastest.
Arguments:
- theta_cube: bfloat16 [32, 90, 4096], P(('ta', 'tb')), may hold values from -20 to 20, as said below
- station_permutation_map: int32 [128], replicated, may hold values from 0 to 127, each once
- station_bathymetry_group: int32 [4096], replicated, may hold values from 0 to 15
- baroclinic_basis: bfloat16 [16, 90, 90], replicated, may hold values from -0.625 to 0.625
Outputs:
- anomaly_coef: bfloat16 [90, 32, 4096], P(None, None, ('ta', 'tb'))
Inputs may be any that keep to these rules, and one draw needn't show every extreme that they name: `theta_cube`: temperature is a level-and-column profile plus time variation.
All inputs are finite; a program needn't handle non-finite values.
Results may differ from a plain program's by a relative error of at most 0.001.
Values may be sent and summed in bfloat16 or wider, within the bound.
No kernel may reach another device: no remote copies, remote signals or barrier semaphores. Data moves between devices by JAX's collectives and lax.ppermute only.
A program may use at most 128 MiB of HBM per device.

v0:
```python
import jax
import jax.numpy as jnp
from jax import lax
from jax.sharding import PartitionSpec as P

TILE = 32


def on_device(theta_cube, station_permutation_map, station_bathymetry_group, baroclinic_basis):
    instant_portion, vertical_grid_count, ocean_stations = theta_cube.shape
    classes, _, mode_count = baroclinic_basis.shape
    size_ta = lax.axis_size("ta")
    size_tb = lax.axis_size("tb")
    devices = size_ta * size_tb
    col_dev = ocean_stations // devices
    group_count = ocean_stations // TILE
    owner = lax.axis_index("ta") * size_tb + lax.axis_index("tb")
    grouped = theta_cube.reshape(instant_portion, vertical_grid_count, group_count, TILE)
    regrouped_stations = jnp.take(grouped, station_permutation_map, axis=2).reshape(
        instant_portion, vertical_grid_count, devices, col_dev
    )
    my_groups = lax.dynamic_slice_in_dim(
        station_permutation_map, owner * (col_dev // TILE), col_dev // TILE
    )
    my_columns = (my_groups[:, None] * TILE + jnp.arange(TILE, dtype=jnp.int32)[None, :]).reshape(
        col_dev
    )
    local_category = jnp.take(station_bathymetry_group, my_columns, axis=0)
    one_hot = (local_category[:, None] == jnp.arange(classes, dtype=jnp.int32)[None, :]).astype(
        jnp.bfloat16
    )
    per_column = jnp.dot(
        one_hot,
        baroclinic_basis.reshape(classes, vertical_grid_count * mode_count),
        preferred_element_type=jnp.float32,
    )
    per_column = per_column.astype(jnp.bfloat16).reshape(col_dev, vertical_grid_count, mode_count)
    shaped = regrouped_stations.reshape(
        1, 1, instant_portion, vertical_grid_count, size_ta, size_tb, col_dev
    )
    moved = lax.all_to_all(
        lax.all_to_all(shaped, "ta", split_axis=4, concat_axis=0, tiled=True),
        "tb",
        split_axis=5,
        concat_axis=1,
        tiled=True,
    )
    gathered = moved.reshape(devices * instant_portion, vertical_grid_count, col_dev)
    modal_amplitude = jnp.einsum(
        "btq,qtf->fbq", gathered, per_column, preferred_element_type=jnp.float32
    )
    mean_coef = jnp.mean(modal_amplitude, axis=1, keepdims=True)
    return (modal_amplitude - mean_coef).astype(jnp.bfloat16)


def solution(mesh):
    return jax.shard_map(
        on_device,
        mesh=mesh,
        in_specs=(P(("ta", "tb"), None, None), P(), P(), P()),
        out_specs=P(None, None, ("ta", "tb")),
        check_vma=False,
    )
```

profile of v0, /device:TPU:0, one launch (start us, length us, event | category | flops | bytes accessed | tf_op | source)
XLA Modules:
  0.0 55.1 jit_solution(2020896969279646395)
XLA Ops:
  0.0 0.0 copy-start
  0.0 0.7 %compare_select_fusion = s32[128]{0:T(128)S(1)} fusion(s32[128]{0:T(128)} %param.5), kind=kLoop, calls=%fused_computation.14 | loop fusion | flops 384 | bytes 1024 | tf_op jit(solution)/shard_map/jit(_take)/jit(_where)/select_n | solution.py:19
  0.7 0.7 %compare_and_fusion = pred[128]{0:T(512)(128)(4,1)S(1)} fusion(s32[128]{0:T(128)} %param.5), kind=kLoop, calls=%fused_computation.18 | loop fusion | flops 768 | bytes 640 | tf_op jit(solution)/shard_map/jit(_take)/and | solution.py:19
  1.3 1.6 %copy.14 = bf16[1,90,4096]{1,2,0:T(8,128)(2,1)S(1)} copy(bf16[1,90,4096]{2,1,0:T(8,128)(2,1)} %param.4) | data formatting | bytes 1474560 | tf_op args[0]
  2.9 0.1 broadcast_in_dim.30
  3.1 0.1 broadcast_in_dim.31
  3.2 0.1 broadcast_in_dim.32
  3.3 0.8 %gather_fusion.1 = bf16[128,90,32]{1,2,0:T(8,128)(2,1)S(1)} fusion(bf16[90,128,32]{0,2,1:T(8,128)(2,1)S(1)} %bitcast.28, s32[1024]{0:T(1024)S(1)} %pad_clamp_fusion), kind=kCustom, calls=%fused_computation.1 | custom fusion | bytes 1475072 | tf_op jit(solution)/shard_map/jit(_take)/gather | solution.py:19
  4.0 0.7 %broadcast_select_fusion = bf16[1,1,1,90,4,8,128]{3,6,5,4,2,1,0:T(8,128)(2,1)S(1)} fusion(bf16[1,1,1,90,4,8,128]{3,6,5,4,2,1,0:T(8,128)(2,1)S(1)} %bitcast.29, pred[4,8,128]{2,1,0:T(8,128)(4,1)S(1)} %broadcast_in_dim.32), kind=kLoop, calls=%fused_computation.8 | loop fusion | flops 368640 | bytes 1478656 | tf_op jit(solution)/shard_map/jit(_take)/select_n | solution.py:19
  4.8 0.7 %copy.15 = bf16[1,1,1,90,4,8,128]{6,5,3,2,1,0,4:T(8,128)(2,1)S(1)} copy(bf16[1,1,1,90,4,8,128]{3,6,5,4,2,1,0:T(8,128)(2,1)S(1)} %broadcast_select_fusion) | data formatting | bytes 1474560 | tf_op jit(solution)/shard_map/jit(_take)/select_n | solution.py:19
  5.4 0.0 copy-start.2
  5.5 0.0 copy-start.1
  5.5 15.3 %all_to_all.33 = bf16[1,1,1,90,4,8,128]{6,5,3,2,1,0,4:T(8,128)(2,1)S(1)} all-to-all(bf16[1,1,1,90,4,8,128]{6,5,3,2,1,0,4:T(8,128)(2,1)S(1)} %copy.15), channel_id=1, replica_groups=mesh['ta'=4,'tb'=8] {'ta'}, dimensions={4} | all-to-all | bytes 1474560 | tf_op jit(solution)/shard_map/all_to_all | solution.py:42
  20.7 1.1 %copy.16 = bf16[4,1,1,90,1,8,128]{6,0,4,3,2,1,5:T(4,128)(2,1)} copy(bf16[4,1,1,90,1,8,128]{6,5,3,0,4,2,1:T(8,128)(2,1)S(1)} %bitcast.30) | data formatting | bytes 1474560 | tf_op jit(solution)/shard_map/all_to_all | solution.py:42
  21.9 5.8 %all-to-all-start.1 = ((bf16[4,1,1,90,1,8,128]{6,0,4,3,2,1,5:T(4,128)(2,1)}), bf16[4,1,1,90,1,8,128]{6,0,4,3,2,1,5:T(4,128)(2,1)}, u32[]{:S(2)}, u32[]{:S(2)}) async-start(bf16[4,1,1,90,1,8,128]{6,0,4,3,2,1,5:T(4,128)(2,1)} %copy.16), calls=%async_computation.1 | async-start | bytes 1474560 | tf_op jit(solution)/shard_map/all_to_all | solution.py:41
  27.7 0.0 copy-done.2
  27.7 0.1 dynamic-slice_multiply_fusion
  27.8 0.1 iota_add_fusion
  27.9 0.1 add.78
  28.0 0.1 add.75
  28.0 0.0 copy-done.1
  28.0 0.1 copy.13
  28.2 0.5 reshape.91
  28.7 0.0 copy-done
  28.7 1.1 %gather_fusion = s32[128]{0:T(128)S(1)} fusion(s32[4096]{0:T(1024)S(1)} %copy-done, s32[1024]{0:T(1024)S(1)} %pad_clamp_fusion.1), kind=kCustom, calls=%fused_computation | custom fusion | bytes 1536 | tf_op jit(solution)/shard_map/jit(_take)/gather | solution.py:28
  29.9 1.3 %convolution_convert_fusion = bf16[128,8100]{0,1:T(8,128)(2,1)S(1)} fusion(bf16[16,8100]{1,0:T(8,128)(2,1)S(1)} %reshape.91, s32[128]{0:T(128)S(1)} %and_select_fusion), kind=kOutput, calls=%fused_computation.2 | convolution fusion | flops 34216448 | bytes 2333312 | tf_op jit(solution)/shard_map/dot_general | solution.py:32
  31.2 1.9 %reshape.92 = bf16[128,90,90]{0,2,1:T(8,128)(2,1)} reshape(bf16[128,8100]{0,1:T(8,128)(2,1)S(1)} %convolution_convert_fusion) | data formatting | bytes 4147200 | tf_op jit(solution)/shard_map/reshape | solution.py:37
  33.1 3.6 %copy.18 = bf16[128,90,90]{2,1,0:T(8,128)(2,1)S(1)} copy(bf16[128,90,90]{0,2,1:T(8,128)(2,1)} %reshape.92) | data formatting | bytes 4147200 | tf_op jit(solution)/shard_map/reshape | solution.py:37
  36.7 10.1 %all-to-all-done.1 = bf16[4,1,1,90,1,8,128]{6,0,4,3,2,1,5:T(4,128)(2,1)} async-done(((bf16[4,1,1,90,1,8,128]{6,0,4,3,2,1,5:T(4,128)(2,1)}), bf16[4,1,1,90,1,8,128]{6,0,4,3,2,1,5:T(4,128)(2,1)}, u32[]{:S(2)}, u32[]{:S(2)}) %all-to-all-start.1) | async-done | bytes 737312 | tf_op jit(solution)/shard_map/all_to_all | solution.py:41
  46.8 3.7 %copy.17 = bf16[4,8,1,1,90,1,1,128]{4,1,0,7,6,5,3,2:T(8,128)(2,1)} copy(bf16[4,8,1,1,90,1,1,128]{7,0,4,1,6,5,3,2:T(4,128)(2,1)} %bitcast.8) | data formatting | bytes 1474560 | tf_op jit(solution)/shard_map/all_to_all | solution.py:41
  50.4 2.2 %bitcast_reduce_fusion = (f32[90,128]{0,1:T(8,128)S(1)}, f32[128,90,32]{1,2,0:T(8,128)S(1)}) fusion(bf16[128,90,90]{2,1,0:T(8,128)(2,1)S(1)} %copy.18, bf16[4,8,1,1,90,1,1,128]{4,1,0,7,6,5,3,2:T(8,128)(2,1)} %copy.17), kind=kOutput, calls=%fused_computation.4 | convolution fusion | flops 66712320 | bytes 4331520 | tf_op jit(solution)/shard_map/btq,qtf->fbq/dot_general | solution.py:49
  52.6 0.3 fusion
  53.0 2.1 %copy.19 = bf16[90,32,128]{2,1,0:T(8,128)(2,1)} copy(bf16[90,32,128]{0,1,2:T(8,128)(2,1)S(1)} %fusion) | data formatting | bytes 1474560 | tf_op jit(solution)/shard_map/convert_element_type | solution.py:53
  (5 shorter events, 0.0 us)
Async XLA Ops:
  0.0 28.7 %copy-start = (s32[4096]{0:T(1024)S(1)}, s32[4096]{0:T(1024)}, u32[]{:S(2)}) copy-start(s32[4096]{0:T(1024)} %param.6) | copy-start | bytes 49156
  5.4 22.3 %copy-start.2 = (s32[128]{0:T(128)S(1)}, s32[128]{0:T(128)}, u32[]{:S(2)}) copy-start(s32[128]{0:T(128)} %param.5) | copy-start | bytes 1540
  5.5 22.6 %copy-start.1 = (bf16[16,90,90]{2,0,1:T(8,128)(2,1)S(1)}, bf16[16,90,90]{2,0,1:T(8,128)(2,1)}, u32[]{:S(2)}) copy-start(bf16[16,90,90]{2,0,1:T(8,128)(2,1)} %param.7) | copy-start | bytes 777604
  21.9 24.9 %all-to-all-start.1 = ((bf16[4,1,1,90,1,8,128]{6,0,4,3,2,1,5:T(4,128)(2,1)}), bf16[4,1,1,90,1,8,128]{6,0,4,3,2,1,5:T(4,128)(2,1)}, u32[]{:S(2)}, u32[]{:S(2)}) async-start(bf16[4,1,1,90,1,8,128]{6,0,4,3,2,1,5:T(4,128)(2,1)} %copy.16), calls=%async_computation.1 | async-start | bytes 1474560 | tf_op jit(solution)/shard_map/all_to_all | solution.py:41
where the time goes:
time: 55.5 us; the launch traced here: 55.1 us
  local copies, waits for them, and re-layouts  17.6 us (32%)
  blocking collectives  15.3 us (28%)
  waiting for transfers between devices  10.1 us (18%)
  starting transfers between devices  5.83 us (11%)
  matrix products  3.49 us (6%)
  other arithmetic  2.57 us (5%)
    all_to_all x1, blocking collectives, on_device(): lax.all_to_all(shaped, 'ta', split_axis=4, concat_axis=0, tiled=True)  15.3 us
    all_to_all x1, waiting for transfers between devices, on_device(): lax.all_to_all(lax.all_to_all(shaped, 'ta', split_axis=4, concat_axis=0,...  10.1 us
    all_to_all x1, starting transfers between devices, on_device(): lax.all_to_all(lax.all_to_all(shaped, 'ta', split_axis=4, concat_axis=0,...  5.83 us
    reshape x2, local copies, waits for them, and re-layouts, on_device(): per_column.astype(jnp.bfloat16)  5.47 us
    all_to_all x1, local copies, waits for them, and re-layouts, on_device(): lax.all_to_all(lax.all_to_all(shaped, 'ta', split_axis=4, concat_axis=0,...  3.66 us
    dot_general x1, matrix products, on_device(): jnp.einsum('btq,qtf->fbq', gathered, per_column, preferred_element_type=j...  2.16 us
    convert_element_type x1, local copies, waits for them, and re-layouts, on_device(): return (modal_amplitude - mean_coef).astype(jnp.bfloat16)  2.1 us
    unnamed x8, local copies, waits for them, and re-layouts  1.71 us
  transfers between devices with their start and end apart: 1, of which 1 were waited for; matrix products, arithmetic and copies ran while one was open for 16% of the time, Pallas kernels for 0%

commit v1 on v0

v1 whole, which is shorter than its diff:
```python
import jax
import jax.numpy as jnp
from jax import lax
from jax.experimental import pallas as pl
from jax.experimental.pallas import tpu as pltpu
from jax.sharding import PartitionSpec as P

TILE = 32
LANES = 128
PACK = 16


def round_up(value, step):
    return -(-value // step) * step


def column_block(read, perm_ref, first_group, lane_group, tiles):
    block = None
    for slot in range(tiles):
        group = perm_ref[first_group + slot]
        piece = read(group // tiles)
        piece = pltpu.roll(piece, lax.rem(slot + tiles - lax.rem(group, tiles), tiles) * TILE, 1)
        block = piece if block is None else jnp.where(lane_group == slot, piece, block)
    return block


def regroup_kernel(perm_ref, theta_ref, out_ref):
    dests, levels_pad, width = out_ref.shape
    levels = theta_ref.shape[0]
    tiles = width // TILE
    lane_group = lax.broadcasted_iota(jnp.int32, (levels, width), 1) // TILE

    def read(index):
        return theta_ref[:, pl.ds(pl.multiple_of(index * width, width), width)].astype(jnp.float32)

    def one(dest, carry):
        block = column_block(read, perm_ref, dest * tiles, lane_group, tiles)
        out_ref[dest, 0:levels, :] = block.astype(out_ref.dtype)
        out_ref[dest, levels:levels_pad, :] = jnp.zeros((levels_pad - levels, width), out_ref.dtype)
        return carry

    lax.fori_loop(0, dests, one, 0)


def modes_kernel(perm_ref, owner_ref, classes_ref, basis_ref, recv_ref, out_ref, weight_ref, coef_ref):
    snaps, levels_pad, width = recv_ref.shape
    classes, levels, modes = basis_ref.shape
    tiles = width // TILE
    modes_pad = weight_ref.shape[0]
    lane_group = lax.broadcasted_iota(jnp.int32, (8, width), 1) // TILE

    def read(index):
        return jnp.broadcast_to(classes_ref[pl.ds(index, 1), :], (8, width))

    mine = column_block(read, perm_ref, owner_ref[0] * tiles, lane_group, tiles)
    mine = jnp.broadcast_to(mine[0:1].astype(jnp.float32), (levels_pad, width)).astype(jnp.bfloat16)

    for c in range(classes):
        square = jnp.pad(basis_ref[c].astype(jnp.float32), ((0, LANES - levels), (0, LANES - modes)))
        square = square.T[0:modes_pad, 0:levels_pad]
        weight_ref[:, c * levels_pad:(c + 1) * levels_pad] = square.astype(jnp.bfloat16)

    group = 2

    def one(step, total):
        cols = []
        for t in range(group):
            value = recv_ref[step * group + t]
            cols.append(jnp.concatenate(
                [jnp.where(mine == jnp.bfloat16(c), value, jnp.bfloat16(0)) for c in range(classes)], axis=0))
        both = jnp.concatenate(cols, axis=1)
        coef = jnp.dot(weight_ref[...], both, preferred_element_type=jnp.float32)
        for t in range(group):
            piece = coef[0:modes, t * width:(t + 1) * width]
            total = total + piece
            coef_ref[pl.ds(step * group + t, modes, stride=snaps), :] = piece
        return total

    total = lax.fori_loop(0, snaps // group, one, jnp.zeros((modes, width), jnp.float32))
    mean = total * (1.0 / snaps)
    for m in range(modes):
        rows = coef_ref[m * snaps:(m + 1) * snaps, :]
        out_ref[m] = (rows - mean[m:m + 1]).astype(out_ref.dtype)


def on_device(theta_cube, station_permutation_map, station_bathymetry_group, baroclinic_basis):
    instants, levels, columns = theta_cube.shape
    classes, _, modes = baroclinic_basis.shape
    devices = lax.axis_size("ta") * lax.axis_size("tb")
    width = columns // devices
    snaps = devices * instants
    levels_pad = round_up(levels, PACK)
    modes_pad = round_up(modes, PACK)
    owner = (lax.axis_index("ta") * lax.axis_size("tb") + lax.axis_index("tb")).astype(jnp.int32)
    smem = pl.BlockSpec(memory_space=pltpu.SMEM)
    vmem = pl.BlockSpec(memory_space=pltpu.VMEM)
    regrouped = pl.pallas_call(
        regroup_kernel,
        out_shape=jax.ShapeDtypeStruct((devices, levels_pad, width), theta_cube.dtype),
        in_specs=[smem, vmem],
        out_specs=vmem,
    )(station_permutation_map, theta_cube.reshape(levels, columns))
    moved = lax.all_to_all(regrouped, ("ta", "tb"), split_axis=0, concat_axis=0, tiled=True)
    return pl.pallas_call(
        modes_kernel,
        out_shape=jax.ShapeDtypeStruct((modes, snaps, width), jnp.bfloat16),
        in_specs=[smem, smem, vmem, vmem, vmem],
        out_specs=vmem,
        scratch_shapes=[
            pltpu.VMEM((modes_pad, classes * levels_pad), jnp.bfloat16),
            pltpu.VMEM((modes * snaps, width), jnp.float32),
        ],
    )(station_permutation_map, owner.reshape(1), station_bathymetry_group.reshape(-1, width), baroclinic_basis, moved)


def solution(mesh):
    return jax.shard_map(
        on_device,
        mesh=mesh,
        in_specs=(P(("ta", "tb"), None, None), P(), P(), P()),
        out_specs=P(None, None, ("ta", "tb")),
        check_vma=False,
    )
```

time: 55.5 us -> 43.3 us (0.78)
  local copies, waits for them, and re-layouts: 17.6 us -> 1.73 us
  blocking collectives: 15.3 us -> 0 us
  Pallas kernels: 0 us -> 13 us
  waiting for transfers between devices: 10.1 us -> 21 us
  matrix products: 3.49 us -> 0 us
  other arithmetic: 2.57 us -> 0 us
  starting transfers between devices: 5.83 us -> 7.33 us
    all_to_all x1 -> x0, blocking collectives: 15.3 us -> none  [on_device(): lax.all_to_all(shaped, 'ta', split_axis=4, concat_axis=0, tiled=True)]
    pallas_call x0 -> x2, Pallas kernels: none -> 13 us  [the longest x1 7.5 us: on_device(): pl.pallas_call(modes_kernel, out_shape=jax.ShapeDtypeStruct((modes, snaps...]
    all_to_all x1, waiting for transfers between devices: 10.1 us -> 21 us  [on_device(): lax.all_to_all(regrouped, ('ta', 'tb'), split_axis=0, concat_axis=0, tile...]
    reshape x3 -> x0, local copies, waits for them, and re-layouts: 5.97 us -> none  [the longest x2 5.47 us: on_device(): per_column.astype(jnp.bfloat16)]
    all_to_all x2 -> x0, local copies, waits for them, and re-layouts: 4.81 us -> none  [the longest x1 3.66 us: on_device(): lax.all_to_all(lax.all_to_all(shaped, 'ta', split_axis=4, concat_axis=0,...]
    dot_general x2 -> x0, matrix products: 3.49 us -> none  [the longest x1 2.16 us: on_device(): jnp.einsum('btq,qtf->fbq', gathered, per_column, preferred_element_type=j...]
    convert_element_type x1 -> x0, local copies, waits for them, and re-layouts: 2.1 us -> none  [on_device(): return (modal_amplitude - mean_coef).astype(jnp.bfloat16)]
    gather x2 -> x0, local copies, waits for them, and re-layouts: 1.91 us -> none  [the longest x1 1.15 us: on_device(): local_category = jnp.take(station_bathymetry_group, my_columns, axis=0)]
  transfers between devices with their start and end apart: 1 -> 1, of which waited for: 1 -> 1; matrix products, arithmetic and copies ran while one was open for 16% -> 2% of each run, Pallas kernels for 0% -> 0%
where the time goes in v1:
time: 43.3 us; the launch traced here: 43 us
  waiting for transfers between devices  21 us (48%)
  Pallas kernels  13 us (30%)
  starting transfers between devices  7.33 us (17%)
  local copies, waits for them, and re-layouts  1.73 us (4%)
    all_to_all x1, waiting for transfers between devices, on_device(): lax.all_to_all(regrouped, ('ta', 'tb'), split_axis=0, concat_axis=0, tile...  21 us
    pallas_call x1, Pallas kernels, on_device(): pl.pallas_call(modes_kernel, out_shape=jax.ShapeDtypeStruct((modes, snaps...  7.5 us
    all_to_all x1, starting transfers between devices, on_device(): lax.all_to_all(regrouped, ('ta', 'tb'), split_axis=0, concat_axis=0, tile...  7.33 us
    pallas_call x1, Pallas kernels, on_device(): pl.pallas_call(regroup_kernel, out_shape=jax.ShapeDtypeStruct((devices, l...  5.47 us
    unnamed x5, local copies, waits for them, and re-layouts  1.73 us
  transfers between devices with their start and end apart: 1, of which 1 were waited for; matrix products, arithmetic and copies ran while one was open for 2% of the time, Pallas kernels for 0%

profile of v1, /device:TPU:0, one launch (start us, length us, event | category | flops | bytes accessed | tf_op | source)
XLA Modules:
  0.0 43.0 jit_solution(10587218721075298246)
XLA Ops:
  0.0 5.5 %shard_map.46 = bf16[32,96,128]{2,1,0:T(8,128)(2,1)} custom-call(s32[128]{0:T(128)} %perm_ref.3, bf16[90,4096]{1,0:T(8,128)(2,1)} %bitcast.3), custom_call_target="tpu_custom_call" | custom-call | tf_op jit(solution)/shard_map/pallas_call | solution.py:97
  5.5 0.0 copy-start.1
  5.5 7.3 %all-to-all-start = ((bf16[32,96,128]{2,1,0:T(8,128)(2,1)}), bf16[32,96,128]{2,1,0:T(8,128)(2,1)S(1)}, u32[]{:S(2)}, u32[]{:S(2)}) async-start(bf16[32,96,128]{2,1,0:T(8,128)(2,1)} %shard_map.46), calls=%async_computation | async-start | bytes 1572864 | tf_op jit(solution)/shard_map/all_to_all | solution.py:103
  12.8 0.0 copy-done.1
  12.8 0.8 %copy.5.basis_ref = bf16[16,90,90]{2,1,0:T(8,128)(2,1)} copy(bf16[16,90,90]{2,0,1:T(8,128)(2,1)S(1)} %copy-done.1) | data formatting | bytes 518400 | tf_op args[3]
  13.7 21.0 %all-to-all-done.recv_ref = bf16[32,96,128]{2,1,0:T(8,128)(2,1)S(1)} async-done(((bf16[32,96,128]{2,1,0:T(8,128)(2,1)}), bf16[32,96,128]{2,1,0:T(8,128)(2,1)S(1)}, u32[]{:S(2)}, u32[]{:S(2)}) %all-to-all-start) | async-done | bytes 786464 | tf_op jit(solution)/shard_map/all_to_all | solution.py:103
  34.7 0.0 copy-start
  34.7 0.9 %copy-done = bf16[32,96,128]{2,1,0:T(8,128)(2,1)} copy-done((bf16[32,96,128]{2,1,0:T(8,128)(2,1)}, bf16[32,96,128]{2,1,0:T(8,128)(2,1)S(1)}, u32[]{:S(2)}) %copy-start) | copy-done | bytes 786456
  35.6 7.5 %shard_map.47 = bf16[90,32,128]{2,1,0:T(8,128)(2,1)} custom-call(s32[128]{0:T(128)} %perm_ref.3, s32[1]{0:T(128)} %bitcast.owner_ref, s32[32,128]{1,0:T(8,128)} %bitcast.4, bf16[16,90,90]{2,1,0:T(8,128)(2,1)} %copy.5.basis_ref, bf16[32,96,128]{2,1,0:T(8,128)(2,1)} %copy-done), custom_call_target="tpu_custom_call" | custom-call | tf_op jit(solution)/shard_map/pallas_call | solution.py:104
Async XLA Ops:
  5.5 7.3 %copy-start.1 = (bf16[16,90,90]{2,0,1:T(8,128)(2,1)S(1)}, bf16[16,90,90]{2,0,1:T(8,128)(2,1)}, u32[]{:S(2)}) copy-start(bf16[16,90,90]{2,0,1:T(8,128)(2,1)} %param.7) | copy-start | bytes 777604
  5.5 29.2 %all-to-all-start = ((bf16[32,96,128]{2,1,0:T(8,128)(2,1)}), bf16[32,96,128]{2,1,0:T(8,128)(2,1)S(1)}, u32[]{:S(2)}, u32[]{:S(2)}) async-start(bf16[32,96,128]{2,1,0:T(8,128)(2,1)} %shard_map.46), calls=%async_computation | async-start | bytes 1572864 | tf_op jit(solution)/shard_map/all_to_all | solution.py:103
  34.7 0.9 %copy-start = (bf16[32,96,128]{2,1,0:T(8,128)(2,1)}, bf16[32,96,128]{2,1,0:T(8,128)(2,1)S(1)}, u32[]{:S(2)}) copy-start(bf16[32,96,128]{2,1,0:T(8,128)(2,1)S(1)} %all-to-all-done.recv_ref) | copy-start | bytes 2359300
